TPU v7x, 32 devices: a whole 2x2x4 slice. The times are simulated.
32 devices in a mesh: dp: 4 (over y, x), row: 4 (over z), col: 2 (over core).
Axes of the slice: x: 2, y: 2, z: 4, core: 2. Of those that a mesh axis runs over, the one named last changes fastest.
Arguments:
- block_input: bfloat16 [192, 197, 384], P(('dp', 'row', 'col')), may hold values from -6 to 6
- first_norm_scale: float32 [384], P('row'), may hold values from 0.5 to 1.5
- first_norm_bias: float32 [384], P('row'), may hold values from -1.5 to 1.5
- attn_weight: bfloat16 [6, 384, 256], P('col', 'row'), may hold values from -1.2247449 to 1.2247449
- qv_bias: float32 [2, 384], P(None, 'col'), may hold values from -2.5 to 2.5
- out_bias: float32 [384], P('row'), may hold values from -2.5 to 2.5
- second_norm_scale: float32 [384], P('row'), may hold values from 0.5 to 1.5
- second_norm_bias: float32 [384], P('row'), may hold values from -1.5 to 1.5
- up_weight: bfloat16 [384, 1536], P('row', 'col'), may hold values from -0.3125 to 0.3125
- up_bias: float32 [1536], P('col'), may hold values from -2.5 to 2.5
- down_weight: bfloat16 [384, 1536], P('row', 'col'), may hold values from -0.15625 to 0.15625
- down_bias: float32 [384], P('row'), may hold values from -2.5 to 2.5
- cotangent: bfloat16 [192, 197, 384], P(('dp', 'row', 'col')), may hold values from -6 to 6
Outputs:
- block_output: bfloat16 [192, 197, 384], P(('dp', 'row', 'col'))
- d_x: float32 [192, 197, 384], P(('dp', 'row', 'col'))
- d_ln1_gain: float32 [384], P('row')
- d_ln1_shift: float32 [384], P('row')
- d_attn_weight: float32 [6, 384, 256], P('col', 'row')
- d_qv_bias: float32 [2, 384], P(None, 'col')
- d_out_bias: float32 [384], P('row')
- d_ln2_gain: float32 [384], P('row')
- d_ln2_shift: float32 [384], P('row')
- d_up_weight: float32 [384, 1536], P('row', 'col')
- d_up_bias: float32 [1536], P('col')
- d_down_weight: float32 [384, 1536], P('row', 'col')
- d_down_bias: float32 [384], P('row')
All inputs are finite; a program needn't handle non-finite values.
Results may differ from a plain program's by a relative error of at most 0.013.
Values may be sent and summed in bfloat16 or wider, within the bound.
A program may use at most 448 MiB of HBM per device.

v0:
```python
import math
import jax
import jax.numpy as jnp
from jax import lax
from jax.sharding import PartitionSpec as P

SEQ = 197
HD = 64
EPS = 1e-06
ROOT_HALF = 0.7071067811865476
INV_ROOT_TWO_PI = 0.3989422804014327


def gelu_parts(u):
    cdf = 0.5 * (1.0 + jax.scipy.special.erf(u * ROOT_HALF))
    return (u * cdf, cdf + u * jnp.exp(-0.5 * u * u) * INV_ROOT_TWO_PI)


def row_sum_values(pair):
    return lax.psum((pair[0], pair[1]), "row")


def layer_norm_forward(input_value, scale_factor, offset_bias, feature_width):
    partial_sum_values = row_sum_values(
        (jnp.sum(input_value, -1), jnp.sum(input_value * input_value, -1))
    )
    row_average = partial_sum_values[0] / feature_width
    var = partial_sum_values[1] / feature_width - row_average * row_average
    inverse_deviation = lax.rsqrt(var + EPS)[..., None]
    normalized_input = (input_value - row_average[..., None]) * inverse_deviation
    return (
        normalized_input,
        inverse_deviation,
        (normalized_input * scale_factor + offset_bias).astype(jnp.bfloat16),
    )


def layer_norm_backward(
    incoming_gradient, normalized_input, inverse_deviation, scale_factor, feature_width
):
    normalized_gradient = incoming_gradient * scale_factor
    partial_sum_values = row_sum_values(
        (jnp.sum(normalized_gradient, -1), jnp.sum(normalized_gradient * normalized_input, -1))
    )
    return inverse_deviation * (
        normalized_gradient
        - partial_sum_values[0][..., None] / feature_width
        - normalized_input * (partial_sum_values[1][..., None] / feature_width)
    )


def gather_cols(values):
    return lax.all_gather(values, "col", axis=0, tiled=True)


def gather_rows(values):
    return lax.all_gather(values, "row", axis=0, tiled=True)


def project_in(whole_rows, weight):
    mine = lax.all_to_all(whole_rows, "row", split_axis=0, concat_axis=2, tiled=True)
    full_weight = lax.all_gather(weight, "row", axis=0, tiled=True)
    return jnp.dot(mine, full_weight, preferred_element_type=jnp.float32)


def project_out(whole_rows, weight):
    return lax.psum_scatter(
        jnp.dot(whole_rows, weight, preferred_element_type=jnp.float32),
        "col",
        scatter_dimension=0,
        tiled=True,
    )


def back_to_middle(whole_grad, weight):
    mine = lax.all_to_all(whole_grad, "row", split_axis=0, concat_axis=2, tiled=True)
    full_weight = lax.all_gather(weight, "row", axis=1, tiled=True)
    return lax.dot_general(
        mine, full_weight, (((2,), (1,)), ((), ())), preferred_element_type=jnp.float32
    )


def back_to_input(whole_grad, weight):
    return lax.psum_scatter(
        lax.dot_general(
            whole_grad, weight, (((2,), (1,)), ((), ())), preferred_element_type=jnp.float32
        ),
        "col",
        scatter_dimension=0,
        tiled=True,
    )


def token_product(left, incoming_gradient):
    return lax.dot_general(
        left, incoming_gradient, (((0, 1), (0, 1)), ((), ())), preferred_element_type=jnp.float32
    )


def token_sum(incoming_gradient):
    return jnp.sum(incoming_gradient, axis=(0, 1), dtype=jnp.float32)


def sum_weights(grads):
    return (
        lax.psum(grads[0].astype(jnp.bfloat16), "dp").astype(jnp.float32),
        lax.psum(grads[1].astype(jnp.bfloat16), "dp").astype(jnp.float32),
        lax.psum(grads[2].astype(jnp.bfloat16), "dp").astype(jnp.float32),
        lax.psum(grads[3].astype(jnp.bfloat16), "dp").astype(jnp.float32),
        lax.psum(grads[4].astype(jnp.bfloat16), "dp").astype(jnp.float32),
        lax.psum(grads[5].astype(jnp.bfloat16), "dp").astype(jnp.float32),
        lax.psum(grads[6].astype(jnp.bfloat16), "dp").astype(jnp.float32),
    )


def sum_norms(grads):
    return lax.psum((grads[0], grads[1], grads[2], grads[3]), ("dp", "col"))


def attend_block(inputs):
    query, keys, values = inputs
    scale = 1.0 / math.sqrt(query.shape[-1])
    scores = jnp.einsum("bqhd,bkhd->bhqk", query, keys, preferred_element_type=jnp.float32) * scale
    top = jnp.max(scores, -1, keepdims=True)
    lse = top + jnp.log(jnp.sum(jnp.exp(scores - top), -1, keepdims=True))
    probs = jnp.exp(scores - lse).astype(jnp.bfloat16)
    out = jnp.einsum("bhqk,bkhd->bqhd", probs, values, preferred_element_type=jnp.float32)
    return (out.astype(jnp.bfloat16), lse)


def attend_back_block(inputs):
    query, keys, values, lse, dout = inputs
    scale = 1.0 / math.sqrt(query.shape[-1])
    scores = jnp.einsum("bqhd,bkhd->bhqk", query, keys, preferred_element_type=jnp.float32) * scale
    probs = jnp.exp(scores - lse)
    probs_b = probs.astype(jnp.bfloat16)
    dvals = jnp.einsum("bhqk,bqhd->bkhd", probs_b, dout, preferred_element_type=jnp.float32)
    dprob = jnp.einsum("bqhd,bkhd->bhqk", dout, values, preferred_element_type=jnp.float32)
    delta = jnp.sum(probs * dprob, -1, keepdims=True)
    dsb = (probs * (dprob - delta)).astype(jnp.bfloat16)
    dquery = jnp.einsum("bhqk,bkhd->bqhd", dsb, keys, preferred_element_type=jnp.float32) * scale
    dkeys = jnp.einsum("bhqk,bqhd->bkhd", dsb, query, preferred_element_type=jnp.float32) * scale
    return (dquery.astype(jnp.bfloat16), dkeys.astype(jnp.bfloat16), dvals.astype(jnp.bfloat16))


def local(
    block_input,
    first_norm_scale,
    first_norm_bias,
    attn_weight,
    qv_bias,
    out_bias,
    second_norm_scale,
    second_norm_bias,
    up_weight,
    up_bias,
    down_weight,
    down_bias,
    cotangent,
):
    split_input, split_cotangent = (
        lax.all_to_all(block_input, "row", split_axis=2, concat_axis=0, tiled=True),
        lax.all_to_all(cotangent, "row", split_axis=2, concat_axis=0, tiled=True),
    )
    head_count = attn_weight.shape[0]
    feat_rows = attn_weight.shape[1]
    feat_cols = head_count * HD
    feature_width = feat_rows * lax.axis_size("row")
    qkv_local = (
        attn_weight[:, :, : 3 * HD]
        .reshape(head_count, feat_rows, 3, HD)
        .transpose(1, 2, 0, 3)
        .reshape(feat_rows, 3 * feat_cols)
    )
    out_local = attn_weight[:, :, 3 * HD :].transpose(0, 2, 1).reshape(feat_cols, feat_rows)
    down_local = down_weight.T
    input_as_float = split_input.astype(jnp.float32)
    first_normalized_input, first_inverse_deviation, first_normed_output = layer_norm_forward(
        input_as_float, first_norm_scale, first_norm_bias, feature_width
    )
    whole1 = gather_cols(first_normed_output)
    qkv = project_in(whole1, qkv_local)
    images_mine = qkv.shape[0]
    bias_three = jnp.stack([qv_bias[0], jnp.zeros_like(qv_bias[0]), qv_bias[1]])
    qkv = qkv.reshape(images_mine, SEQ, 3, feat_cols) + bias_three
    group = math.gcd(images_mine, 6)
    nblocks = images_mine // group
    split_shape = (nblocks, group, SEQ, head_count, HD)
    query = qkv[:, :, 0].astype(jnp.bfloat16).reshape(split_shape)
    keys = qkv[:, :, 1].astype(jnp.bfloat16).reshape(split_shape)
    values = qkv[:, :, 2].astype(jnp.bfloat16).reshape(split_shape)
    attn, lse = lax.map(attend_block, (query, keys, values))
    attn_flat = attn.reshape(images_mine, SEQ, feat_cols)
    attn_whole = gather_rows(attn_flat)
    hidden_input = input_as_float + project_out(attn_whole, out_local) + out_bias
    second_normalized_input, second_inverse_deviation, second_normed_output = layer_norm_forward(
        hidden_input, second_norm_scale, second_norm_bias, feature_width
    )
    whole2 = gather_cols(second_normed_output)
    pre = project_in(whole2, up_weight) + up_bias
    act, slope = gelu_parts(pre)
    act_b = act.astype(jnp.bfloat16)
    act_whole = gather_rows(act_b)
    y_out = (hidden_input + project_out(act_whole, down_local) + down_bias).astype(jnp.bfloat16)
    grad_whole = gather_cols(split_cotangent)
    g_down_w = token_product(grad_whole, act_whole)
    g_down_b = token_sum(grad_whole)
    dpre = (back_to_middle(grad_whole, down_local) * slope).astype(jnp.bfloat16)
    dpre_whole = gather_rows(dpre)
    g_up_w = token_product(whole2, dpre_whole)
    g_up_b = token_sum(dpre_whole)
    second_activation_grad = back_to_input(dpre_whole, up_weight)
    second_norm_scale_grad = jnp.sum(second_activation_grad * second_normalized_input, (0, 1))
    g_ln2_s = jnp.sum(second_activation_grad, (0, 1))
    hidden_gradient = split_cotangent.astype(jnp.float32) + layer_norm_backward(
        second_activation_grad,
        second_normalized_input,
        second_inverse_deviation,
        second_norm_scale,
        feature_width,
    )
    dhb = hidden_gradient.astype(jnp.bfloat16)
    dh_whole = gather_cols(dhb)
    g_out_w = token_product(attn_whole, dh_whole)
    g_out_b = token_sum(dh_whole)
    dout = back_to_middle(dh_whole, out_local).astype(jnp.bfloat16).reshape(split_shape)
    dquery, dkeys, dvals = lax.map(attend_back_block, (query, keys, values, lse, dout))
    dqkv = jnp.stack(
        [
            dquery.reshape(images_mine, SEQ, feat_cols),
            dkeys.reshape(images_mine, SEQ, feat_cols),
            dvals.reshape(images_mine, SEQ, feat_cols),
        ],
        2,
    ).reshape(images_mine, SEQ, 3 * feat_cols)
    dqkv_whole = gather_rows(dqkv)
    g_qkv_w = token_product(whole1, dqkv_whole)
    bias_sums = token_sum(dqkv_whole).reshape(3, feat_cols)
    g_qv_b = jnp.stack([bias_sums[0], bias_sums[2]])
    packed_qkv = (
        g_qkv_w.reshape(feat_rows, 3, head_count, HD)
        .transpose(2, 0, 1, 3)
        .reshape(head_count, feat_rows, 3 * HD)
    )
    packed_out = g_out_w.reshape(head_count, HD, feat_rows).transpose(0, 2, 1)
    g_attn = jnp.concatenate([packed_qkv, packed_out], 2)
    first_activation_grad = back_to_input(dqkv_whole, qkv_local)
    first_norm_scale_grad = jnp.sum(first_activation_grad * first_normalized_input, (0, 1))
    g_ln1_s = jnp.sum(first_activation_grad, (0, 1))
    output_input_gradient = hidden_gradient + layer_norm_backward(
        first_activation_grad,
        first_normalized_input,
        first_inverse_deviation,
        first_norm_scale,
        feature_width,
    )
    totals = sum_weights((g_attn, g_qv_b, g_out_b, g_up_w, g_up_b, g_down_w, g_down_b))
    norms = sum_norms((first_norm_scale_grad, g_ln1_s, second_norm_scale_grad, g_ln2_s))
    y_back, dx_back = (
        lax.all_to_all(
            y_out.astype(jnp.float32).astype(jnp.bfloat16),
            "row",
            split_axis=0,
            concat_axis=2,
            tiled=True,
        ).astype(jnp.float32),
        lax.all_to_all(
            output_input_gradient.astype(jnp.bfloat16),
            "row",
            split_axis=0,
            concat_axis=2,
            tiled=True,
        ).astype(output_input_gradient.dtype),
    )
    return (
        y_back.astype(jnp.bfloat16),
        dx_back,
        norms[0],
        norms[1],
        totals[0],
        totals[1],
        totals[2],
        norms[2],
        norms[3],
        totals[3],
        totals[4],
        totals[5],
        totals[6],
    )


def solution(mesh):
    placed = (
        P(("dp", "row", "col"), None, None),
        P("row"),
        P("row"),
        P("col", "row", None),
        P(None, "col"),
        P("row"),
        P("row"),
        P("row"),
        P("row", "col"),
        P("col"),
        P("row", "col"),
        P("row"),
        P(("dp", "row", "col"), None, None),
    )
    return jax.shard_map(
        local,
        mesh=mesh,
        in_specs=placed,
        out_specs=(
            P(("dp", "row", "col"), None, None),
            P(("dp", "row", "col"), None, None),
            P("row"),
            P("row"),
            P("col", "row", None),
            P(None, "col"),
            P("row"),
            P("row"),
            P("row"),
            P("row", "col"),
            P("col"),
            P("row", "col"),
            P("row"),
        ),
        check_vma=False,
    )
```

profile of v0, /device:TPU:0, one launch (start us, length us, event | category | flops | bytes accessed | tf_op | source)
XLA Modules:
  0.0 1588.9 jit_solution(12312043903524667726)
XLA Ops:
  9.5 43.1 %all_to_all.126 = bf16[6,197,384]{1,0,2:T(8,128)(2,1)S(1)} all-to-all(bf16[6,197,384]{1,0,2:T(8,128)(2,1)S(1)} %copy.109), channel_id=1, replica_groups=mesh['dp'=4,'row'=4,'col'=2] {'row'}, dimensions={2} | all-to-all | bytes 1815552 | tf_op jit(solution)/shard_map/all_to_all | solution.py:162
  59.8 3.0 copy.111
  62.7 17.6 %all-reduce.4 = (f32[24,197]{1,0:T(8,128)S(1)}, f32[24,197]{1,0:T(8,128)S(1)}) all-reduce(f32[24,197]{1,0:T(8,128)S(1)} %reduce_sum.178, f32[24,197]{1,0:T(8,128)S(1)} %reduce_sum.176), channel_id=1, replica_groups=mesh['dp'=4,'row'=4,'col'=2] {'row'}, use_global_device_ids=true, to_apply=%region_3.0 | all-reduce | flops 9456 | bytes 75648 | tf_op jit(solution)/shard_map/psum | solution.py:20
  82.5 9.3 all-gather.9.cloned.1.call-done
  91.9 4.9 all-to-all-start.1
  97.8 63.3 %all_gather.37 = bf16[384,576]{1,0:T(8,128)(2,1)S(1)} all-gather(bf16[96,576]{1,0:T(8,128)(2,1)S(1)} %copy.117), channel_id=1, replica_groups=mesh['dp'=4,'row'=4,'col'=2] {'row'}, dimensions={0}, use_global_device_ids=true | all-gather | bytes 552960 | tf_op jit(solution)/shard_map/all_gather | solution.py:62
  162.9 4.2 copy.114
  167.1 4.0 reshape.145
  171.1 3.5 add_convert_fusion
  176.2 7.9 while.26
  187.2 80.7 %all_to_all.127 = bf16[6,197,384]{1,0,2:T(8,128)(2,1)} all-to-all(bf16[6,197,384]{1,0,2:T(8,128)(2,1)} %copy.123), channel_id=1, replica_groups=mesh['dp'=4,'row'=4,'col'=2] {'row'}, dimensions={2} | all-to-all | bytes 1815552 | tf_op jit(solution)/shard_map/all_to_all | solution.py:163
  267.9 3.2 copy.148
  271.1 3.4 copy.125
  277.8 24.4 %all-gather.11.cloned.1.call-done = bf16[48,197,192]{1,2,0:T(8,128)(2,1)} async-done(((bf16[12,197,192]{1,2,0:T(8,128)(2,1)}), bf16[48,197,192]{1,2,0:T(8,128)(2,1)}) %all-gather.11.cloned.1.call-update) | async-done | bytes 3631120 | tf_op jit(solution)/shard_map/all_gather | solution.py:57
  302.3 5.3 fusion.86
  307.6 6.2 all-gather.17.cloned.1.call-done
  313.8 4.9 all-to-all-start.5
  318.7 11.0 reduce-scatter.5.cloned.1.call-done
  329.7 5.1 fusion.81
  334.9 48.0 %all-reduce.3 = (f32[24,197]{1,0:T(8,128)}, f32[24,197]{1,0:T(8,128)}) all-reduce(f32[24,197]{1,0:T(8,128)} %get-tuple-element.150, f32[24,197]{1,0:T(8,128)} %get-tuple-element.149), channel_id=1, replica_groups=mesh['dp'=4,'row'=4,'col'=2] {'row'}, use_global_device_ids=true, to_apply=%region_12.13 | all-reduce | flops 9456 | bytes 75648 | tf_op jit(solution)/shard_map/psum | solution.py:20
  384.2 3.2 add_convert_fusion.3
  387.5 11.2 all-gather.13.cloned.1.call-done
  398.7 4.9 all-to-all-start.2
  403.6 65.9 %all_gather.43 = bf16[768,384]{0,1:T(8,128)(2,1)} all-gather(bf16[768,96]{0,1:T(8,128)(2,1)} %bitcast.266), channel_id=1, replica_groups=mesh['dp'=4,'row'=4,'col'=2] {'row'}, dimensions={1}, use_global_device_ids=true | all-gather | bytes 737280 | tf_op jit(solution)/shard_map/all_gather | solution.py:77
  469.5 17.0 %all_gather.40 = bf16[384,768]{1,0:T(8,128)(2,1)} all-gather(bf16[96,768]{1,0:T(8,128)(2,1)} %param.25), channel_id=1, replica_groups=mesh['dp'=4,'row'=4,'col'=2] {'row'}, dimensions={0}, use_global_device_ids=true | all-gather | bytes 737280 | tf_op jit(solution)/shard_map/all_gather | solution.py:62
  486.5 5.5 copy.126
  491.9 5.3 all_to_all.112
  497.3 5.5 copy.121
  502.8 5.3 all_to_all.100
  508.1 5.5 multiply_convert_fusion.1
  513.6 4.8 fusion.63
  518.5 254.0 %all-gather.19.cloned.1.call-done = bf16[48,197,768]{2,1,0:T(8,128)(2,1)} async-done(((bf16[12,197,768]{2,1,0:T(8,128)(2,1)}), bf16[48,197,768]{2,1,0:T(8,128)(2,1)}) %all-gather.19.cloned.1.call-update) | async-done | bytes 14524432 | tf_op jit(solution)/shard_map/all_gather | solution.py:57
  772.5 9.5 fusion.76
  782.1 10.8 reduce-scatter.9.cloned.1.call-done
  792.9 4.1 multiply_reduce_fusion.3
  797.0 21.1 %all-reduce.2 = (f32[24,197]{1,0:T(8,128)}, f32[24,197]{1,0:T(8,128)}) all-reduce(f32[24,197]{1,0:T(8,128)} %get-tuple-element.140, f32[24,197]{1,0:T(8,128)} %get-tuple-element.146), channel_id=1, replica_groups=mesh['dp'=4,'row'=4,'col'=2] {'row'}, use_global_device_ids=true, to_apply=%region_18.19 | all-reduce | flops 9456 | bytes 75648 | tf_op jit(solution)/shard_map/psum | solution.py:20
  819.5 4.7 fusion.80
  824.2 9.3 all-gather.21.cloned.1.call-done
  833.5 4.9 all-to-all-start.6
  839.9 60.5 %all_gather.46 = bf16[192,384]{0,1:T(8,128)(2,1)} all-gather(bf16[192,96]{0,1:T(8,128)(2,1)} %copy.128), channel_id=1, replica_groups=mesh['dp'=4,'row'=4,'col'=2] {'row'}, dimensions={1}, use_global_device_ids=true | all-gather | bytes 184320 | tf_op jit(solution)/shard_map/all_gather | solution.py:77
  900.4 5.5 copy.127
  905.9 5.3 all_to_all.116
  911.2 3.4 convolution_convert_fusion
  918.1 17.9 %while.27 = (s32[]{:T(128)}, bf16[2,6,197,3,64]{2,4,3,1,0:T(8,128)(2,1)}, bf16[2,6,197,3,64]{2,4,3,1,0:T(8,128)(2,1)}, bf16[2,6,197,3,64]{2,4,3,1,0:T(8,128)(2,1...) while((s32[]{:T(128)}, ...), condition=%wide.region_21.22_spmd, body=%wide.region_19.21_spmd.sunk | while | flops 456593600 | bytes 55074784 | solution.py:227
  938.4 3.7 copy.133
  942.8 213.1 %all-gather.23.cloned.1.call-done = bf16[48,197,576]{2,1,0:T(8,128)(2,1)} async-done(((bf16[12,197,576]{2,1,0:T(8,128)(2,1)}), bf16[48,197,576]{2,1,0:T(8,128)(2,1)}) %all-gather.23.cloned.1.call-update) | async-done | bytes 10893328 | tf_op jit(solution)/shard_map/all_gather | solution.py:57
  1155.9 11.7 fusion.87
  1168.0 241.0 %all-gather.15.cloned.1.call-done = bf16[48,197,768]{2,1,0:T(8,128)(2,1)} async-done(((bf16[12,197,768]{2,1,0:T(8,128)(2,1)}), bf16[48,197,768]{2,1,0:T(8,128)(2,1)}) %all-gather.15.cloned.1.call-update) | async-done | bytes 14524432 | tf_op jit(solution)/shard_map/all_gather | solution.py:57
  1409.0 11.9 fusion.78
  1422.8 8.4 fusion.70
  1431.2 4.5 multiply_reduce_fusion.4
  1435.7 18.1 %all-reduce.1 = (f32[24,197]{1,0:T(8,128)}, f32[24,197]{1,0:T(8,128)}) all-reduce(f32[24,197]{1,0:T(8,128)} %get-tuple-element.142, f32[24,197]{1,0:T(8,128)} %get-tuple-element.145), channel_id=1, replica_groups=mesh['dp'=4,'row'=4,'col'=2] {'row'}, use_global_device_ids=true, to_apply=%region_26.27 | all-reduce | flops 9456 | bytes 75648 | tf_op jit(solution)/shard_map/psum | solution.py:20
  1456.6 7.5 add_convert_fusion.1
  1464.0 3.5 all-to-all-start.3
  1467.6 8.1 fusion.67
  1475.7 4.3 fusion.71
  1480.0 12.8 all-to-all-done.3
  1492.8 4.3 all-to-all-start.7
  1497.3 7.1 fusion.69
  1511.3 7.4 reduce_sum.191
  1519.8 6.6 reduce.5
  1526.5 10.1 all-reduce.5
  1538.7 17.3 %all-reduce.9.cloned.1.call-done = (bf16[3,96,256]{1,2,0:T(8,128)(2,1)}, bf16[96,768]{1,0:T(8,128)(2,1)}, bf16[96,768]{1,0:T(8,128)(2,1)}) async-done(((bf16[3,96,256]{1,2,0:T(8,128)(2,1)}, bf16[96,768]{1,0:T(8,128)(2,1)}, bf16[96,768]{1,0:T(8,128)(2,1)}), (bf16[3,96,256]{1,2,0:T(8,128)(2,1)}, bf16[96,768]{1,0:T(8,128)(2,1)}, bf16[96,768]{1,0:T(8,128)(2,1)})) %all-reduce.9.cloned.1.call-update) | async-done | bytes 442384 | tf_op jit(solution)/shard_map/psum | solution.py:106
  1561.1 12.6 all-reduce
  (213 shorter events, 87.6 us)
Async XLA Ops:
  7.2 84.7 %all-gather.9.cloned.1.call-start = ((), (), s32[]{:S(2)}) async-start(), calls=%async_computation.12 | async-start | bytes 3538944 | tf_op jit(solution)/shard_map/all_gather | solution.py:53
  55.3 4.4 copy-start.3
  59.7 21.2 %copy-start.31 = (f32[96]{0:T(128)S(1)}, f32[96]{0:T(128)}, u32[]{:S(2)}) copy-start(f32[96]{0:T(128)} %param.18) | copy-start | bytes 1156
  59.7 21.2 %copy-start.38 = (f32[96]{0:T(128)S(1)}, f32[96]{0:T(128)}, u32[]{:S(2)}) copy-start(f32[96]{0:T(128)} %param.19) | copy-start | bytes 1156
  62.7 19.8 %copy-start.1 = (f32[4,6,197,96]{2,3,1,0:T(8,128)}, f32[4,6,197,96]{2,3,1,0:T(8,128)S(1)}, u32[]{:S(2)}) copy-start(f32[4,6,197,96]{2,3,1,0:T(8,128)S(1)} %copy.111) | copy-start | bytes 5446660
  82.5 14.2 copy-start.25
  91.9 69.6 %all-to-all-start.1 = ((bf16[48,197,96]{1,2,0:T(8,128)(2,1)}), bf16[48,197,96]{1,2,0:T(8,128)(2,1)S(1)}, u32[]{:S(2)}, u32[]{:S(2)}) async-start(bf16[48,197,96]{1,2,0:T(8,128)(2,1)} %all-gather.9.cloned.1.call-done), calls=%async_computation.1 | async-start | bytes 4718592 | tf_op jit(solution)/shard_map/all_to_all | solution.py:61
  96.7 64.6 %copy-start.35 = (f32[2,192]{1,0:T(2,128)S(1)}, f32[2,192]{1,0:T(2,128)}, u32[]{:S(2)}) copy-start(f32[2,192]{1,0:T(2,128)} %param.21) | copy-start | bytes 4612
  96.7 205.5 %all-gather.11.cloned.1.call-start = ((), (), s32[]{:S(2)}) async-start(), calls=%async_computation.13 | async-start | bytes 5898240 | tf_op jit(solution)/shard_map/all_gather | solution.py:57
  161.4 1.5 copy-start.7
  176.9 0.8 copy-start.26
  177.0 1.3 copy-start.14
  177.8 1.3 copy-start.27
  179.1 1.1 copy-start.15
  180.9 1.3 copy-start.14
  181.7 1.3 copy-start.27
  183.0 1.1 copy-start.15
  184.1 129.7 %all-gather.17.cloned.1.call-start = ((), (), s32[]{:S(2)}) async-start(), calls=%async_computation.18 | async-start | bytes 3538944 | tf_op jit(solution)/shard_map/all_gather | solution.py:53
  274.6 55.2 %reduce-scatter.5.cloned.1.call-start = ((), (), s32[]{:S(2)}) async-start(), calls=%async_computation.14 | async-start | bytes 7077888 | tf_op jit(solution)/shard_map/reduce_scatter | solution.py:67
  307.6 22.1 %copy-start.39 = (f32[96]{0:T(128)S(1)}, f32[96]{0:T(128)}, u32[]{:S(2)}) copy-start(f32[96]{0:T(128)} %param.22) | copy-start | bytes 1156
  313.8 73.6 %all-to-all-start.5 = ((bf16[48,197,96]{1,2,0:T(8,128)(2,1)}), bf16[48,197,96]{1,2,0:T(8,128)(2,1)}, u32[]{:S(2)}, u32[]{:S(2)}) async-start(bf16[48,197,96]{1,2,0:T(8,128)(2,1)} %all-gather.17.cloned.1.call-done), calls=%async_computation.7 | async-start | bytes 4718592 | tf_op jit(solution)/shard_map/all_to_all | solution.py:76
  318.7 65.5 %copy-start.30 = (f32[96]{0:T(128)S(1)}, f32[96]{0:T(128)}, u32[]{:S(2)}) copy-start(f32[96]{0:T(128)} %param.23) | copy-start | bytes 1156
  318.7 65.5 %copy-start.40 = (f32[96]{0:T(128)S(1)}, f32[96]{0:T(128)}, u32[]{:S(2)}) copy-start(f32[96]{0:T(128)} %param.24) | copy-start | bytes 1156
  318.7 80.0 %all-gather.13.cloned.1.call-start = ((), (), s32[]{:S(2)}) async-start(), calls=%async_computation.15 | async-start | bytes 3538944 | tf_op jit(solution)/shard_map/all_gather | solution.py:53
  398.7 98.6 %all-to-all-start.2 = ((bf16[48,197,96]{1,2,0:T(8,128)(2,1)}), bf16[48,197,96]{1,2,0:T(8,128)(2,1)}, u32[]{:S(2)}, u32[]{:S(2)}) async-start(bf16[48,197,96]{1,2,0:T(8,128)(2,1)} %all-gather.13.cloned.1.call-done), calls=%async_computation.3 | async-start | bytes 4718592 | tf_op jit(solution)/shard_map/all_to_all | solution.py:61
  403.6 368.9 %all-gather.19.cloned.1.call-start = ((), (), s32[]{:S(2)}) async-start(), calls=%async_computation.19 | async-start | bytes 18432000 | tf_op jit(solution)/shard_map/all_gather | solution.py:57
  502.8 5.3 copy-start.41
  508.1 5.5 copy-start.16
  508.1 5.5 copy-start.21
  518.5 274.4 %reduce-scatter.9.cloned.1.call-start = ((), (), s32[]{:S(2)}) async-start(), calls=%async_computation.20 | async-start | bytes 7077888 | tf_op jit(solution)/shard_map/reduce_scatter | solution.py:84
  782.0 51.5 %all-gather.21.cloned.1.call-start = ((), (), s32[]{:S(2)}) async-start(), calls=%async_computation.21 | async-start | bytes 3538944 | tf_op jit(solution)/shard_map/all_gather | solution.py:53
  833.5 66.9 %all-to-all-start.6 = ((bf16[48,197,96]{1,2,0:T(8,128)(2,1)}), bf16[48,197,96]{1,2,0:T(8,128)(2,1)}, u32[]{:S(2)}, u32[]{:S(2)}) async-start(bf16[48,197,96]{1,2,0:T(8,128)(2,1)} %all-gather.21.cloned.1.call-done), calls=%async_computation.9 | async-start | bytes 4718592 | tf_op jit(solution)/shard_map/all_to_all | solution.py:76
  838.4 317.5 %all-gather.23.cloned.1.call-start = ((), (), s32[]{:S(2)}) async-start(), calls=%async_computation.22 | async-start | bytes 15360000 | tf_op jit(solution)/shard_map/all_gather | solution.py:57
  918.8 1.3 copy-start.2
  918.9 1.6 copy-start.8
  921.3 1.1 copy-start.9
  922.4 1.3 copy-start.10
  923.7 1.3 copy-start.12
  925.0 1.1 copy-start.11
  926.0 1.0 copy-start.13
  927.8 1.3 copy-start.2
  927.8 1.6 copy-start.8
  930.2 1.1 copy-start.9
  931.4 1.3 copy-start.10
  932.6 1.3 copy-start.12
  933.9 1.1 copy-start.11
  935.0 1.0 copy-start.13
  942.1 213.7 %copy-start.18 = (bf16[96,3,3,64]{0,3,2,1:T(8,128)(2,1)S(1)}, bf16[96,3,3,64]{0,3,2,1:T(8,128)(2,1)}, u32[]{:S(2)}) copy-start(bf16[96,3,3,64]{0,3,2,1:T(8,128)(2,1)} %copy-done.17) | copy-start | bytes 331780
  942.1 466.9 %all-gather.15.cloned.1.call-start = ((), (), s32[]{:S(2)}) async-start(), calls=%async_computation.16 | async-start | bytes 18432000 | tf_op jit(solution)/shard_map/all_gather | solution.py:57
  942.7 488.5 %reduce-scatter.11.cloned.1.call-start = ((), (), s32[]{:S(2)}) async-start(), calls=%async_computation.23 | async-start | bytes 7077888 | tf_op jit(solution)/shard_map/reduce_scatter | solution.py:84
  1167.5 241.5 %copy-start.22 = (bf16[96,768]{1,0:T(8,128)(2,1)S(1)}, bf16[96,768]{1,0:T(8,128)(2,1)}, u32[]{:S(2)}) copy-start(bf16[96,768]{1,0:T(8,128)(2,1)} %param.27) | copy-start | bytes 442372
  1167.6 289.0 %reduce-scatter.7.cloned.1.call-start = ((), (), s32[]{:S(2)}) async-start(), calls=%async_computation.17 | async-start | bytes 7077888 | tf_op jit(solution)/shard_map/reduce_scatter | solution.py:67
  1421.0 1.8 copy-start.6
  1422.8 8.4 copy-start.32
  1431.2 25.4 %copy-start = (f32[24,197,96]{1,2,0:T(8,128)S(1)}, f32[24,197,96]{1,2,0:T(8,128)}, u32[]{:S(2)}) copy-start(f32[24,197,96]{1,2,0:T(8,128)} %get-tuple-element.202) | copy-start | bytes 5446660
  1431.2 25.4 %copy-start.5 = (bf16[4,6,197,96]{2,3,1,0:T(8,128)(2,1)S(1)}, bf16[4,6,197,96]{2,3,1,0:T(8,128)(2,1)}, u32[]{:S(2)}) copy-start(bf16[4,6,197,96]{2,3,1,0:T(8,128)(2,1)} %copy.125) | copy-start | bytes 2723332
  1464.0 28.8 %all-to-all-start.3 = ((bf16[24,197,96]{1,2,0:T(8,128)(2,1)}), bf16[24,197,96]{1,2,0:T(8,128)(2,1)S(1)}, u32[]{:S(2)}, u32[]{:S(2)}) async-start(bf16[24,197,96]{1,2,0:T(8,128)(2,1)} %get-tuple-element.211), calls=%async_computation.5 | async-start | bytes 2359296 | tf_op jit(solution)/shard_map/all_to_all | solution.py:260
  1467.6 8.1 copy-start.4
  1492.8 84.3 %all-to-all-start.7 = ((bf16[24,197,96]{1,2,0:T(8,128)(2,1)}), bf16[24,197,96]{1,2,0:T(8,128)(2,1)}, u32[]{:S(2)}, u32[]{:S(2)}) async-start(bf16[24,197,96]{1,2,0:T(8,128)(2,1)} %get-tuple-element.210), calls=%async_computation.11 | async-start | bytes 2359296 | tf_op jit(solution)/shard_map/all_to_all | solution.py:267
  1497.1 58.9 %all-reduce.9.cloned.1.call-start = ((), (), s32[]{:S(2)}) async-start(), calls=%async_computation.24 | async-start | bytes 983040 | tf_op jit(solution)/shard_map/psum | solution.py:106
  1519.7 6.7 copy-start.36
  1519.8 6.7 copy-start.37
  1519.8 41.3 %copy-start.33 = (f32[96]{0:T(128)S(1)}, f32[96]{0:T(128)}, u32[]{:S(2)}) copy-start(f32[96]{0:T(128)} %get-tuple-element.141) | copy-start | bytes 1156
  1519.8 41.3 %copy-start.34 = (f32[96]{0:T(128)S(1)}, f32[96]{0:T(128)}, u32[]{:S(2)}) copy-start(f32[96]{0:T(128)} %get-tuple-element.148) | copy-start | bytes 1156
  (8 other events, 5.1 us)
Sparse Core Ops, SparseCore 0:
  82.6 9.1 all-gather.8
  184.2 117.9 all-gather.10
  303.8 9.9 all-gather.16
  316.0 13.7 reduce-scatter.4
  387.6 11.0 all-gather.12
  518.6 253.8 all-gather.18
  782.1 10.7 reduce-scatter.8
  824.3 9.1 all-gather.20
  942.2 213.5 all-gather.22
  1157.3 251.7 all-gather.14
  1411.3 10.7 reduce-scatter.10
  1424.3 13.8 reduce-scatter.6
  1508.7 47.2 all-reduce.8
where the time goes:
time: 1600 us; the launch traced here: 1590 us
  waiting for transfers between devices  821 us (51%)
  blocking collectives  458 us (29%)
  local copies, waits for them, and re-layouts  104 us (6%)
  matrix products  94.4 us (6%)
  other arithmetic  68 us (4%)
  starting transfers between devices  28.4 us (2%)
    all_gather x4, waiting for transfers between devices, gather_rows(): return lax.all_gather(values, 'row', axis=0, tiled=True)  732 us
    all_gather x2, blocking collectives, back_to_middle(): full_weight = lax.all_gather(weight, 'row', axis=1, tiled=True)  126 us
    psum x4, blocking collectives, row_sum_values(): return lax.psum((pair[0], pair[1]), 'row')  105 us
    all_to_all x1, blocking collectives, local(): lax.all_to_all(cotangent, 'row', split_axis=2, concat_axis=0, tiled=True)  80.7 us
    all_gather x2, blocking collectives, project_in(): full_weight = lax.all_gather(weight, 'row', axis=0, tiled=True)  80.3 us
    all_to_all x1, blocking collectives, local(): lax.all_to_all(block_input, 'row', split_axis=2, concat_axis=0, tiled=True)  43.1 us
    all_gather x4, waiting for transfers between devices, gather_cols(): return lax.all_gather(values, 'col', axis=0, tiled=True)  36.1 us
  transfers between devices with their start and end apart: 19, of which 12 were waited for; matrix products, arithmetic and copies ran while one was open for 8% of the time, Pallas kernels for 0%

commit v1 on v0

--- a/solution.py
+++ b/solution.py
@@ -9,6 +9,17 @@
 EPS = 1e-06
 ROOT_HALF = 0.7071067811865476
 INV_ROOT_TWO_PI = 0.3989422804014327
+
+
+def gather_around(array, axis, dim):
+    ways = lax.axis_size(axis)
+    pieces = [array]
+    for far in range(1, ways):
+        pieces.append(
+            lax.ppermute(pieces[far - 1], axis, [(d, (d - 1) % ways) for d in range(ways)])
+        )
+    line = jnp.concatenate(pieces, axis=dim)
+    return jnp.roll(line, lax.axis_index(axis) * array.shape[dim], axis=dim)
 
 
 def gelu_parts(u):
@@ -59,7 +70,7 @@
 
 def project_in(whole_rows, weight):
     mine = lax.all_to_all(whole_rows, "row", split_axis=0, concat_axis=2, tiled=True)
-    full_weight = lax.all_gather(weight, "row", axis=0, tiled=True)
+    full_weight = gather_around(weight, "row", 0)
     return jnp.dot(mine, full_weight, preferred_element_type=jnp.float32)
 
 

time: 1600 us -> 1600 us (level)
  blocking collectives: 458 us -> 340 us
  waiting for transfers between devices: 821 us -> 921 us
  starting transfers between devices: 28.4 us -> 48 us
    ppermute x0 -> x6, waiting for transfers between devices: none -> 98.1 us  [gather_around(): lax.ppermute(pieces[far - 1], axis, [(d, (d - 1) % ways) for d in range(w...]
    all_gather x2 -> x0, blocking collectives: 80.3 us -> none  [project_in(): full_weight = lax.all_gather(weight, 'row', axis=0, tiled=True)]
    all_gather x2, blocking collectives: 126 us -> 88.2 us  [back_to_middle(): full_weight = lax.all_gather(weight, 'row', axis=1, tiled=True)]
    ppermute x0 -> x6, starting transfers between devices: none -> 19.9 us  [gather_around(): lax.ppermute(pieces[far - 1], axis, [(d, (d - 1) % ways) for d in range(w...]
  transfers between devices with their start and end apart: 19 -> 25, of which waited for: 12 -> 17; matrix products, arithmetic and copies ran while one was open for 8% -> 8% of each run, Pallas kernels for 0% -> 0%
where the time goes in v1:
time: 1600 us; the launch traced here: 1590 us
  waiting for transfers between devices  921 us (58%)
  blocking collectives  340 us (21%)
  local copies, waits for them, and re-layouts  109 us (7%)
  matrix products  94.5 us (6%)
  other arithmetic  68 us (4%)
  starting transfers between devices  48 us (3%)
    all_gather x4, waiting for transfers between devices, gather_rows(): return lax.all_gather(values, 'row', axis=0, tiled=True)  734 us
    psum x4, blocking collectives, row_sum_values(): return lax.psum((pair[0], pair[1]), 'row')  105 us
    ppermute x6, waiting for transfers between devices, gather_around(): lax.ppermute(pieces[far - 1], axis, [(d, (d - 1) % ways) for d in range(w...  98.1 us
    all_gather x2, blocking collectives, back_to_middle(): full_weight = lax.all_gather(weight, 'row', axis=1, tiled=True)  88.2 us
    all_to_all x1, blocking collectives, local(): lax.all_to_all(cotangent, 'row', split_axis=2, concat_axis=0, tiled=True)  81.2 us
    all_to_all x1, blocking collectives, local(): lax.all_to_all(block_input, 'row', split_axis=2, concat_axis=0, tiled=True)  43.1 us
    all_gather x4, waiting for transfers between devices, gather_cols(): return lax.all_gather(values, 'col', axis=0, tiled=True)  36.1 us
  transfers between devices with their start and end apart: 25, of which 17 were waited for; matrix products, arithmetic and copies ran while one was open for 8% of the time, Pallas kernels for 0%

profile of v1, /device:TPU:0, one launch (start us, length us, event | category | flops | bytes accessed | tf_op | source)
XLA Modules:
  0.0 1595.0 jit_solution(7012503005836382189)
XLA Ops:
  9.5 43.1 %all_to_all.126 = bf16[6,197,384]{1,0,2:T(8,128)(2,1)S(1)} all-to-all(bf16[6,197,384]{1,0,2:T(8,128)(2,1)S(1)} %copy.107), channel_id=1, replica_groups=mesh['dp'=4,'row'=4,'col'=2] {'row'}, dimensions={2} | all-to-all | bytes 1815552 | tf_op jit(solution)/shard_map/all_to_all | solution.py:173
  62.7 17.6 %all-reduce.4 = (f32[24,197]{1,0:T(8,128)S(1)}, f32[24,197]{1,0:T(8,128)S(1)}) all-reduce(f32[24,197]{1,0:T(8,128)S(1)} %reduce_sum.178, f32[24,197]{1,0:T(8,128)S(1)} %reduce_sum.176), channel_id=1, replica_groups=mesh['dp'=4,'row'=4,'col'=2] {'row'}, use_global_device_ids=true, to_apply=%region_3.0 | all-reduce | flops 9456 | bytes 75648 | tf_op jit(solution)/shard_map/psum | solution.py:31
  82.6 9.3 all-gather.9.cloned.1.call-done
  91.9 4.9 all-to-all-start.1
  96.9 3.9 collective-permute-start
  100.8 37.7 %collective-permute-done = bf16[96,576]{0,1:T(8,128)(2,1)S(1)} collective-permute-done((bf16[96,576]{0,1:T(8,128)(2,1)S(1)}, bf16[96,576]{0,1:T(8,128)(2,1)S(1)}, u32[]{:S(2)}, u32[]{:S(2)}) %collective-permute-start) | collective-permute-done | bytes 110624 | tf_op jit(solution)/shard_map/ppermute | solution.py:19
  138.5 4.3 collective-permute-start.1
  142.9 15.0 collective-permute-done.1
  158.6 4.7 collective-permute-done.2
  167.2 4.2 copy.112
  171.5 4.0 reshape.145
  175.5 3.5 add_convert_fusion
  180.6 7.9 while.26
  191.4 81.2 %all_to_all.127 = bf16[6,197,384]{1,0,2:T(8,128)(2,1)} all-to-all(bf16[6,197,384]{1,0,2:T(8,128)(2,1)} %copy.119), channel_id=1, replica_groups=mesh['dp'=4,'row'=4,'col'=2] {'row'}, dimensions={2} | all-to-all | bytes 1815552 | tf_op jit(solution)/shard_map/all_to_all | solution.py:174
  282.5 24.3 %all-gather.11.cloned.1.call-done = bf16[48,197,192]{1,2,0:T(8,128)(2,1)} async-done(((bf16[12,197,192]{1,2,0:T(8,128)(2,1)}), bf16[48,197,192]{1,2,0:T(8,128)(2,1)}) %all-gather.11.cloned.1.call-update) | async-done | bytes 3631120 | tf_op jit(solution)/shard_map/all_gather | solution.py:68
  306.7 5.3 fusion.88
  312.1 6.3 all-gather.17.cloned.1.call-done
  318.3 4.9 all-to-all-start.5
  323.3 11.0 reduce-scatter.5.cloned.1.call-done
  334.3 5.1 fusion.83
  339.4 48.0 %all-reduce.3 = (f32[24,197]{1,0:T(8,128)}, f32[24,197]{1,0:T(8,128)}) all-reduce(f32[24,197]{1,0:T(8,128)} %get-tuple-element.150, f32[24,197]{1,0:T(8,128)} %get-tuple-element.149), channel_id=1, replica_groups=mesh['dp'=4,'row'=4,'col'=2] {'row'}, use_global_device_ids=true, to_apply=%region_12.13 | all-reduce | flops 9456 | bytes 75648 | tf_op jit(solution)/shard_map/psum | solution.py:31
  392.0 11.2 all-gather.13.cloned.1.call-done
  403.2 4.9 all-to-all-start.2
  408.1 3.8 collective-permute-start.3
  411.9 38.0 %collective-permute-done.3 = bf16[96,768]{1,0:T(8,128)(2,1)S(1)} collective-permute-done((bf16[96,768]{1,0:T(8,128)(2,1)}, bf16[96,768]{1,0:T(8,128)(2,1)S(1)}, u32[]{:S(2)}, u32[]{:S(2)}) %collective-permute-start.3) | collective-permute-done | bytes 147488 | tf_op jit(solution)/shard_map/ppermute | solution.py:19
  449.9 4.2 collective-permute-start.4
  454.2 27.7 %all_gather.35 = bf16[768,384]{0,1:T(8,128)(2,1)} all-gather(bf16[768,96]{0,1:T(8,128)(2,1)} %bitcast.268), channel_id=1, replica_groups=mesh['dp'=4,'row'=4,'col'=2] {'row'}, dimensions={1}, use_global_device_ids=true | all-gather | bytes 737280 | tf_op jit(solution)/shard_map/all_gather | solution.py:88
  491.0 5.5 copy.122
  496.5 5.3 all_to_all.112
  501.8 5.5 copy.117
  507.2 5.3 all_to_all.100
  512.6 5.6 multiply_convert_fusion.1
  518.2 4.8 fusion.63
  523.1 255.8 %all-gather.19.cloned.1.call-done = bf16[48,197,768]{2,1,0:T(8,128)(2,1)} async-done(((bf16[12,197,768]{2,1,0:T(8,128)(2,1)}), bf16[48,197,768]{2,1,0:T(8,128)(2,1)}) %all-gather.19.cloned.1.call-update) | async-done | bytes 14524432 | tf_op jit(solution)/shard_map/all_gather | solution.py:68
  778.9 9.5 fusion.77
  788.4 10.8 reduce-scatter.9.cloned.1.call-done
  799.3 4.1 multiply_reduce_fusion.3
  803.4 20.8 %all-reduce.2 = (f32[24,197]{1,0:T(8,128)}, f32[24,197]{1,0:T(8,128)}) all-reduce(f32[24,197]{1,0:T(8,128)} %get-tuple-element.140, f32[24,197]{1,0:T(8,128)} %get-tuple-element.146), channel_id=1, replica_groups=mesh['dp'=4,'row'=4,'col'=2] {'row'}, use_global_device_ids=true, to_apply=%region_18.19 | all-reduce | flops 9456 | bytes 75648 | tf_op jit(solution)/shard_map/psum | solution.py:31
  825.6 4.7 fusion.82
  830.3 9.3 all-gather.21.cloned.1.call-done
  839.6 4.9 all-to-all-start.6
  846.0 60.5 %all_gather.38 = bf16[192,384]{0,1:T(8,128)(2,1)} all-gather(bf16[192,96]{0,1:T(8,128)(2,1)} %copy.124), channel_id=1, replica_groups=mesh['dp'=4,'row'=4,'col'=2] {'row'}, dimensions={1}, use_global_device_ids=true | all-gather | bytes 184320 | tf_op jit(solution)/shard_map/all_gather | solution.py:88
  906.5 5.4 copy.123
  912.0 5.3 all_to_all.116
  924.2 17.8 %while.27 = (s32[]{:T(128)}, bf16[2,6,197,3,64]{2,4,3,1,0:T(8,128)(2,1)}, bf16[2,6,197,3,64]{2,4,3,1,0:T(8,128)(2,1)}, bf16[2,6,197,3,64]{2,4,3,1,0:T(8,128)(2,1...) while((s32[]{:T(128)}, ...), condition=%wide.region_21.22_spmd, body=%wide.region_19.21_spmd.sunk | while | flops 456593600 | bytes 55074784 | solution.py:238
  944.4 3.7 copy.129
  948.8 213.1 %all-gather.23.cloned.1.call-done = bf16[48,197,576]{2,1,0:T(8,128)(2,1)} async-done(((bf16[12,197,576]{2,1,0:T(8,128)(2,1)}), bf16[48,197,576]{2,1,0:T(8,128)(2,1)}) %all-gather.23.cloned.1.call-update) | async-done | bytes 10893328 | tf_op jit(solution)/shard_map/all_gather | solution.py:68
  1161.9 11.7 fusion.89
  1173.8 241.2 %all-gather.15.cloned.1.call-done = bf16[48,197,768]{2,1,0:T(8,128)(2,1)} async-done(((bf16[12,197,768]{2,1,0:T(8,128)(2,1)}), bf16[48,197,768]{2,1,0:T(8,128)(2,1)}) %all-gather.15.cloned.1.call-update) | async-done | bytes 14524432 | tf_op jit(solution)/shard_map/all_gather | solution.py:68
  1415.0 11.9 fusion.79
  1428.8 8.4 fusion.70
  1437.2 4.5 multiply_reduce_fusion.4
  1441.7 18.1 %all-reduce.1 = (f32[24,197]{1,0:T(8,128)}, f32[24,197]{1,0:T(8,128)}) all-reduce(f32[24,197]{1,0:T(8,128)} %get-tuple-element.142, f32[24,197]{1,0:T(8,128)} %get-tuple-element.145), channel_id=1, replica_groups=mesh['dp'=4,'row'=4,'col'=2] {'row'}, use_global_device_ids=true, to_apply=%region_26.27 | all-reduce | flops 9456 | bytes 75648 | tf_op jit(solution)/shard_map/psum | solution.py:31
  1462.6 7.5 add_convert_fusion.1
  1473.6 8.1 fusion.67
  1481.7 4.3 fusion.71
  1486.0 12.8 all-to-all-done.3
  1498.8 4.3 all-to-all-start.7
  1503.4 7.1 fusion.69
  1517.3 7.4 reduce_sum.191
  1525.8 6.6 reduce.5
  1532.5 10.0 all-reduce.5
  1544.7 17.3 %all-reduce.9.cloned.1.call-done = (bf16[3,96,256]{1,2,0:T(8,128)(2,1)}, bf16[96,768]{1,0:T(8,128)(2,1)}, bf16[96,768]{1,0:T(8,128)(2,1)}) async-done(((bf16[3,96,256]{1,2,0:T(8,128)(2,1)}, bf16[96,768]{1,0:T(8,128)(2,1)}, bf16[96,768]{1,0:T(8,128)(2,1)}), (bf16[3,96,256]{1,2,0:T(8,128)(2,1)}, bf16[96,768]{1,0:T(8,128)(2,1)}, bf16[96,768]{1,0:T(8,128)(2,1)})) %all-reduce.9.cloned.1.call-update) | async-done | bytes 442384 | tf_op jit(solution)/shard_map/psum | solution.py:117
  1567.1 12.6 all-reduce
  (237 shorter events, 118.0 us)
Async XLA Ops:
  7.2 84.7 %all-gather.9.cloned.1.call-start = ((), (), s32[]{:S(2)}) async-start(), calls=%async_computation.12 | async-start | bytes 3538944 | tf_op jit(solution)/shard_map/all_gather | solution.py:64
  55.3 4.4 copy-start.3
  59.7 21.2 %copy-start.34 = (f32[96]{0:T(128)S(1)}, f32[96]{0:T(128)}, u32[]{:S(2)}) copy-start(f32[96]{0:T(128)} %param.18) | copy-start | bytes 1156
  59.7 21.2 %copy-start.41 = (f32[96]{0:T(128)S(1)}, f32[96]{0:T(128)}, u32[]{:S(2)}) copy-start(f32[96]{0:T(128)} %param.19) | copy-start | bytes 1156
  62.7 19.8 %copy-start.1 = (f32[4,6,197,96]{2,3,1,0:T(8,128)}, f32[4,6,197,96]{2,3,1,0:T(8,128)S(1)}, u32[]{:S(2)}) copy-start(f32[4,6,197,96]{2,3,1,0:T(8,128)S(1)} %copy.109) | copy-start | bytes 5446660
  82.5 14.2 copy-start.27
  82.5 60.3 %copy-start.38 = (f32[2,192]{1,0:T(2,128)S(1)}, f32[2,192]{1,0:T(2,128)}, u32[]{:S(2)}) copy-start(f32[2,192]{1,0:T(2,128)} %param.21) | copy-start | bytes 4612
  91.9 73.9 %all-to-all-start.1 = ((bf16[48,197,96]{1,2,0:T(8,128)(2,1)}), bf16[48,197,96]{1,2,0:T(8,128)(2,1)S(1)}, u32[]{:S(2)}, u32[]{:S(2)}) async-start(bf16[48,197,96]{1,2,0:T(8,128)(2,1)} %all-gather.9.cloned.1.call-done), calls=%async_computation.1 | async-start | bytes 4718592 | tf_op jit(solution)/shard_map/all_to_all | solution.py:72
  96.7 210.0 %all-gather.11.cloned.1.call-start = ((), (), s32[]{:S(2)}) async-start(), calls=%async_computation.13 | async-start | bytes 5898240 | tf_op jit(solution)/shard_map/all_gather | solution.py:68
  96.9 68.9 %copy-start.16 = (bf16[96,3,3,64]{0,3,2,1:T(8,128)(2,1)}, bf16[96,3,3,64]{0,3,2,1:T(8,128)(2,1)S(1)}, u32[]{:S(2)}) copy-start(bf16[96,3,3,64]{0,3,2,1:T(8,128)(2,1)S(1)} %copy.114) | copy-start | bytes 331780
  96.9 41.5 %collective-permute-start = (bf16[96,576]{0,1:T(8,128)(2,1)S(1)}, bf16[96,576]{0,1:T(8,128)(2,1)S(1)}, u32[]{:S(2)}, u32[]{:S(2)}) collective-permute-start(bf16[96,576]{0,1:T(8,128)(2,1)S(1)} %bitcast.261), channel_id=1, source_target_pairs={{0,6},{2,0},{4,2},{6,4},{1,7},{3,1},{5,3},{7,5},{8,14},{10,8},{12,... | collective-permute-start | bytes 331784 | tf_op jit(solution)/shard_map/ppermute | solution.py:19
  138.5 19.4 %collective-permute-start.1 = (bf16[96,576]{0,1:T(8,128)(2,1)S(1)}, bf16[96,576]{0,1:T(8,128)(2,1)S(1)}, u32[]{:S(2)}, u32[]{:S(2)}) collective-permute-start(bf16[96,576]{0,1:T(8,128)(2,1)S(1)} %collective-permute-done), channel_id=1, source_target_pairs={{0,6},{2,0},{4,2},{6,4},{1,7},{3,1},{5,3},{7,5},{8,14},{10,8},{12,... | collective-permute-start | bytes 331784 | tf_op jit(solution)/shard_map/ppermute | solution.py:19
  157.9 5.4 collective-permute-start.2
  165.8 1.4 copy-start.7
  171.5 4.0 copy-start.24
  181.3 1.3 copy-start.14
  182.1 1.3 copy-start.29
  185.3 1.3 copy-start.14
  186.1 1.3 copy-start.29
  188.5 129.9 %all-gather.17.cloned.1.call-start = ((), (), s32[]{:S(2)}) async-start(), calls=%async_computation.18 | async-start | bytes 3538944 | tf_op jit(solution)/shard_map/all_gather | solution.py:64
  279.2 55.0 %reduce-scatter.5.cloned.1.call-start = ((), (), s32[]{:S(2)}) async-start(), calls=%async_computation.14 | async-start | bytes 7077888 | tf_op jit(solution)/shard_map/reduce_scatter | solution.py:78
  312.1 22.2 %copy-start.42 = (f32[96]{0:T(128)S(1)}, f32[96]{0:T(128)}, u32[]{:S(2)}) copy-start(f32[96]{0:T(128)} %param.22) | copy-start | bytes 1156
  318.3 73.6 %all-to-all-start.5 = ((bf16[48,197,96]{1,2,0:T(8,128)(2,1)}), bf16[48,197,96]{1,2,0:T(8,128)(2,1)}, u32[]{:S(2)}, u32[]{:S(2)}) async-start(bf16[48,197,96]{1,2,0:T(8,128)(2,1)} %all-gather.17.cloned.1.call-done), calls=%async_computation.7 | async-start | bytes 4718592 | tf_op jit(solution)/shard_map/all_to_all | solution.py:87
  323.2 65.5 %copy-start.33 = (f32[96]{0:T(128)S(1)}, f32[96]{0:T(128)}, u32[]{:S(2)}) copy-start(f32[96]{0:T(128)} %param.23) | copy-start | bytes 1156
  323.2 65.5 %copy-start.43 = (f32[96]{0:T(128)S(1)}, f32[96]{0:T(128)}, u32[]{:S(2)}) copy-start(f32[96]{0:T(128)} %param.24) | copy-start | bytes 1156
  323.2 80.0 %all-gather.13.cloned.1.call-start = ((), (), s32[]{:S(2)}) async-start(), calls=%async_computation.15 | async-start | bytes 3538944 | tf_op jit(solution)/shard_map/all_gather | solution.py:64
  403.2 98.6 %all-to-all-start.2 = ((bf16[48,197,96]{1,2,0:T(8,128)(2,1)}), bf16[48,197,96]{1,2,0:T(8,128)(2,1)}, u32[]{:S(2)}, u32[]{:S(2)}) async-start(bf16[48,197,96]{1,2,0:T(8,128)(2,1)} %all-gather.13.cloned.1.call-done), calls=%async_computation.3 | async-start | bytes 4718592 | tf_op jit(solution)/shard_map/all_to_all | solution.py:72
  408.1 370.8 %all-gather.19.cloned.1.call-start = ((), (), s32[]{:S(2)}) async-start(), calls=%async_computation.19 | async-start | bytes 18432000 | tf_op jit(solution)/shard_map/all_gather | solution.py:68
  408.1 41.8 %collective-permute-start.3 = (bf16[96,768]{1,0:T(8,128)(2,1)}, bf16[96,768]{1,0:T(8,128)(2,1)S(1)}, u32[]{:S(2)}, u32[]{:S(2)}) collective-permute-start(bf16[96,768]{1,0:T(8,128)(2,1)} %param.25), channel_id=1, source_target_pairs={{0,6},{2,0},{4,2},{6,4},{1,7},{3,1},{5,3},{7,5},{8,14},{10,8},{12,... | collective-permute-start | bytes 442376 | tf_op jit(solution)/shard_map/ppermute | solution.py:19
  449.9 32.8 %collective-permute-start.4 = (bf16[96,768]{1,0:T(8,128)(2,1)S(1)}, bf16[96,768]{1,0:T(8,128)(2,1)S(1)}, u32[]{:S(2)}, u32[]{:S(2)}) collective-permute-start(bf16[96,768]{1,0:T(8,128)(2,1)S(1)} %collective-permute-done.3), channel_id=1, source_target_pairs={{0,6},{2,0},{4,2},{6,4},{1,7},{3,1},{5,3},{7,5},{8,14},{10,8},{12,... | collective-permute-start | bytes 442376 | tf_op jit(solution)/shard_map/ppermute | solution.py:19
  482.8 6.2 collective-permute-start.5
  507.2 5.3 copy-start.44
  512.6 5.6 copy-start.18
  512.6 5.6 copy-start.22
  523.0 276.3 %reduce-scatter.9.cloned.1.call-start = ((), (), s32[]{:S(2)}) async-start(), calls=%async_computation.20 | async-start | bytes 7077888 | tf_op jit(solution)/shard_map/reduce_scatter | solution.py:95
  788.4 51.3 %all-gather.21.cloned.1.call-start = ((), (), s32[]{:S(2)}) async-start(), calls=%async_computation.21 | async-start | bytes 3538944 | tf_op jit(solution)/shard_map/all_gather | solution.py:64
  839.6 66.9 %all-to-all-start.6 = ((bf16[48,197,96]{1,2,0:T(8,128)(2,1)}), bf16[48,197,96]{1,2,0:T(8,128)(2,1)}, u32[]{:S(2)}, u32[]{:S(2)}) async-start(bf16[48,197,96]{1,2,0:T(8,128)(2,1)} %all-gather.21.cloned.1.call-done), calls=%async_computation.9 | async-start | bytes 4718592 | tf_op jit(solution)/shard_map/all_to_all | solution.py:87
  844.5 317.4 %all-gather.23.cloned.1.call-start = ((), (), s32[]{:S(2)}) async-start(), calls=%async_computation.22 | async-start | bytes 15360000 | tf_op jit(solution)/shard_map/all_gather | solution.py:68
  924.9 1.3 copy-start.2
  924.9 1.6 copy-start.8
  928.5 1.3 copy-start.10
  929.8 1.3 copy-start.12
  933.8 1.3 copy-start.2
  933.8 1.6 copy-start.8
  936.3 1.1 copy-start.9
  937.4 1.3 copy-start.10
  938.7 1.3 copy-start.12
  948.1 213.7 %copy-start.17 = (bf16[96,3,3,64]{0,3,2,1:T(8,128)(2,1)S(1)}, bf16[96,3,3,64]{0,3,2,1:T(8,128)(2,1)}, u32[]{:S(2)}) copy-start(bf16[96,3,3,64]{0,3,2,1:T(8,128)(2,1)} %copy-done.16) | copy-start | bytes 331780
  948.1 466.9 %all-gather.15.cloned.1.call-start = ((), (), s32[]{:S(2)}) async-start(), calls=%async_computation.16 | async-start | bytes 18432000 | tf_op jit(solution)/shard_map/all_gather | solution.py:68
  948.7 488.5 %reduce-scatter.11.cloned.1.call-start = ((), (), s32[]{:S(2)}) async-start(), calls=%async_computation.23 | async-start | bytes 7077888 | tf_op jit(solution)/shard_map/reduce_scatter | solution.py:95
  1173.5 241.5 %copy-start.23 = (bf16[96,768]{1,0:T(8,128)(2,1)S(1)}, bf16[96,768]{1,0:T(8,128)(2,1)}, u32[]{:S(2)}) copy-start(bf16[96,768]{1,0:T(8,128)(2,1)} %param.27) | copy-start | bytes 442372
  1173.6 289.0 %reduce-scatter.7.cloned.1.call-start = ((), (), s32[]{:S(2)}) async-start(), calls=%async_computation.17 | async-start | bytes 7077888 | tf_op jit(solution)/shard_map/reduce_scatter | solution.py:78
  1427.0 1.8 copy-start.6
  1428.8 8.4 copy-start.35
  1437.2 25.4 %copy-start = (f32[24,197,96]{1,2,0:T(8,128)S(1)}, f32[24,197,96]{1,2,0:T(8,128)}, u32[]{:S(2)}) copy-start(f32[24,197,96]{1,2,0:T(8,128)} %get-tuple-element.202) | copy-start | bytes 5446660
  1437.2 25.4 %copy-start.5 = (bf16[4,6,197,96]{2,3,1,0:T(8,128)(2,1)S(1)}, bf16[4,6,197,96]{2,3,1,0:T(8,128)(2,1)}, u32[]{:S(2)}) copy-start(bf16[4,6,197,96]{2,3,1,0:T(8,128)(2,1)} %copy.121) | copy-start | bytes 2723332
  1470.0 28.8 %all-to-all-start.3 = ((bf16[24,197,96]{1,2,0:T(8,128)(2,1)}), bf16[24,197,96]{1,2,0:T(8,128)(2,1)S(1)}, u32[]{:S(2)}, u32[]{:S(2)}) async-start(bf16[24,197,96]{1,2,0:T(8,128)(2,1)} %get-tuple-element.211), calls=%async_computation.5 | async-start | bytes 2359296 | tf_op jit(solution)/shard_map/all_to_all | solution.py:271
  1473.6 8.1 copy-start.4
  1498.8 84.3 %all-to-all-start.7 = ((bf16[24,197,96]{1,2,0:T(8,128)(2,1)}), bf16[24,197,96]{1,2,0:T(8,128)(2,1)}, u32[]{:S(2)}, u32[]{:S(2)}) async-start(bf16[24,197,96]{1,2,0:T(8,128)(2,1)} %get-tuple-element.210), calls=%async_computation.11 | async-start | bytes 2359296 | tf_op jit(solution)/shard_map/all_to_all | solution.py:278
  1503.1 59.0 %all-reduce.9.cloned.1.call-start = ((), (), s32[]{:S(2)}) async-start(), calls=%async_computation.24 | async-start | bytes 983040 | tf_op jit(solution)/shard_map/psum | solution.py:117
  1525.8 6.7 copy-start.39
  1525.8 6.7 copy-start.40
  1525.8 41.3 %copy-start.36 = (f32[96]{0:T(128)S(1)}, f32[96]{0:T(128)}, u32[]{:S(2)}) copy-start(f32[96]{0:T(128)} %get-tuple-element.141) | copy-start | bytes 1156
  1525.8 41.3 %copy-start.37 = (f32[96]{0:T(128)S(1)}, f32[96]{0:T(128)}, u32[]{:S(2)}) copy-start(f32[96]{0:T(128)} %get-tuple-element.148) | copy-start | bytes 1156
  (17 other events, 14.3 us)
Sparse Core Ops, SparseCore 0:
  82.6 9.1 all-gather.8
  188.6 118.0 all-gather.10
  308.3 10.0 all-gather.16
  320.5 13.7 reduce-scatter.4
  392.1 11.0 all-gather.12
  523.1 255.6 all-gather.18
  788.5 10.7 reduce-scatter.8
  830.5 9.1 all-gather.20
  948.3 213.5 all-gather.22
  1163.3 251.7 all-gather.14
  1417.3 10.7 reduce-scatter.10
  1430.3 13.8 reduce-scatter.6
  1514.8 47.2 all-reduce.8
